TPU v7x, 8 devices: a whole 2x2x1 slice. The times are simulated.
8 devices in a mesh: dp: 1 (over z), m3: 2 (over y), m2: 2 (over x), m1: 2 (over core).
Axes of the slice: x: 2, y: 2, z: 1, core: 2. Of those that a mesh axis runs over, the one named last changes fastest.
Arguments:
- volume: bfloat16 [128, 128, 128, 128], P('dp', 'm1', 'm2', 'm3')
- fac_one: bfloat16 [128, 128], replicated
- fac_two: bfloat16 [128, 128], replicated
- fac_three: bfloat16 [128, 128], replicated
- diag_scale: float32 [128, 128, 128], P('m2', 'm1')
Outputs:
- output: bfloat16 [128, 128, 128, 128], P(('dp', 'm3'), 'm2', 'm1')
All inputs are finite; a program needn't handle non-finite values.
Results may differ from a plain program's by a relative error of at most 0.00844248.
Values are sent between devices in bfloat16 or wider.
A program may use at most 1 GiB of HBM per device.

v0:
```python
import jax
import jax.numpy as jnp
from jax import lax
from jax.sharding import PartitionSpec as P


def solution(mesh):
    def local_step(vol_blk, fac_one, fac_two, fac_three, diag_blk):
        full_three = lax.all_to_all(vol_blk, "m3", 0, 3, tiled=True)
        prod_three = lax.dot_general(full_three, fac_three, (((3,), (1,)), ((), ())), preferred_element_type=jnp.float32).astype(jnp.bfloat16)
        full_two = lax.all_to_all(prod_three, "m2", 3, 2, tiled=True)
        prod_two = lax.dot_general(full_two, fac_two, (((2,), (1,)), ((), ())), preferred_element_type=jnp.float32).astype(jnp.bfloat16)
        full_one = lax.all_to_all(prod_two, "m1", 3, 1, tiled=True)
        prod_one = lax.dot_general(full_one, fac_one, (((1,), (1,)), ((), ())), preferred_element_type=jnp.float32).astype(jnp.bfloat16)
        return (diag_blk[None] * prod_one.astype(jnp.float32)).astype(jnp.bfloat16)

    return jax.shard_map(local_step, mesh=mesh, in_specs=(P("dp", "m1", "m2", "m3"), P(), P(), P(), P("m2", "m1", None)), out_specs=P(("dp", "m3"), "m2", "m1", None), check_vma=False)
```

profile of v0, /device:TPU:0, one launch (start us, length us, event | category | flops | bytes accessed | tf_op | source)
XLA Modules:
  0.0 4604.5 jit_solution(10491152277166812971)
XLA Ops:
  0.0 0.0 copy-start
  0.0 177.8 %copy.9 = bf16[128,64,64,64]{3,2,1,0:T(8,128)(2,1)} copy(bf16[128,64,64,64]{0,3,2,1:T(8,128)(2,1)} %param.5) | data formatting | bytes 134217728 | tf_op args[0]
  177.8 112.2 %reshape.4 = bf16[2,2,8388608]{2,1,0:T(2,128)(2,1)} reshape(bf16[128,64,64,64]{3,2,1,0:T(8,128)(2,1)} %copy.9) | data formatting | bytes 134217728
  290.0 783.9 %all_to_all.54 = bf16[2,2,8388608]{2,1,0:T(2,128)(2,1)} all-to-all(bf16[2,2,8388608]{2,1,0:T(2,128)(2,1)} %reshape.4), channel_id=1, replica_groups=mesh['dp'=1,'m3'=2,'m2'=2,'m1'=2] {'m3'}, dimensions={0} | all-to-all | bytes 134217728 | tf_op jit(solution)/shard_map/all_to_all | solution.py:9
  1073.9 172.2 %reshape.5 = bf16[128,64,64,64]{3,2,1,0:T(8,128)(2,1)} reshape(bf16[2,2,8388608]{2,1,0:T(2,128)(2,1)} %all_to_all.54) | data formatting | bytes 134217728
  1246.1 235.7 %copy.21 = bf16[2,64,64,64,64]{4,0,3,2,1:T(2,128)(2,1)} copy(bf16[2,64,64,64,64]{4,3,2,1,0:T(8,128)(2,1)} %bitcast) | data formatting | bytes 134217728 | tf_op jit(solution)/shard_map/all_to_all | solution.py:9
  1481.8 205.5 %all_to_all.42 = bf16[64,64,64,128]{3,2,1,0:T(8,128)(2,1)} reshape(bf16[64,64,64,2,64]{4,3,2,1,0:T(2,128)(2,1)} %bitcast.35) | data formatting | bytes 134217728 | tf_op jit(solution)/shard_map/all_to_all | solution.py:9
  1687.3 0.0 copy-done
  1687.3 47.2 %convolution_convert_fusion.1 = bf16[64,64,64,128]{3,2,1,0:T(8,128)(2,1)} fusion(bf16[64,64,64,128]{3,2,1,0:T(8,128)(2,1)} %all_to_all.42, bf16[128,128]{1,0:T(8,128)(2,1)S(1)} %copy-done), kind=kOutput, calls=%fused_computation.4 | convolution fusion | flops 8623489024 | bytes 134250496 | tf_op jit(solution)/shard_map/dot_general | solution.py:10
  1734.5 177.8 %copy.11 = bf16[64,64,64,128]{2,1,0,3:T(8,128)(2,1)} copy(bf16[64,64,64,128]{3,2,1,0:T(8,128)(2,1)} %convolution_convert_fusion.1) | data formatting | bytes 134217728 | tf_op jit(solution)/shard_map/convert_element_type | solution.py:10
  1912.3 112.2 %reshape.6 = bf16[2,2,8388608]{2,1,0:T(2,128)(2,1)} reshape(bf16[128,64,64,64]{3,2,1,0:T(8,128)(2,1)} %bitcast.27) | data formatting | bytes 134217728
  2024.5 781.7 %all_to_all.55 = bf16[2,2,8388608]{2,1,0:T(2,128)(2,1)} all-to-all(bf16[2,2,8388608]{2,1,0:T(2,128)(2,1)} %reshape.6), channel_id=1, replica_groups=mesh['dp'=1,'m3'=2,'m2'=2,'m1'=2] {'m2'}, dimensions={0} | all-to-all | bytes 134217728 | tf_op jit(solution)/shard_map/all_to_all | solution.py:11
  2806.2 172.2 %reshape.7 = bf16[128,64,64,64]{3,2,1,0:T(8,128)(2,1)} reshape(bf16[2,2,8388608]{2,1,0:T(2,128)(2,1)} %all_to_all.55) | data formatting | bytes 134217728
  2978.4 235.9 %copy.20 = bf16[64,64,64,2,64]{2,3,4,1,0:T(2,128)(2,1)} copy(bf16[64,64,64,2,64]{2,1,0,4,3:T(8,128)(2,1)} %bitcast.4) | data formatting | bytes 134217728 | tf_op jit(solution)/shard_map/all_to_all | solution.py:11
  3214.2 0.0 copy-start.2
  3214.2 205.5 %all_to_all.46 = bf16[64,64,128,64]{2,3,1,0:T(8,128)(2,1)} reshape(bf16[64,64,2,64,64]{3,2,4,1,0:T(2,128)(2,1)} %bitcast.34) | data formatting | bytes 134217728 | tf_op jit(solution)/shard_map/all_to_all | solution.py:11
  3419.7 0.0 copy-done.2
  3419.8 47.2 %convolution_convert_fusion = bf16[64,64,64,128]{3,2,1,0:T(8,128)(2,1)} fusion(bf16[64,64,128,64]{2,3,1,0:T(8,128)(2,1)} %all_to_all.46, bf16[128,128]{1,0:T(8,128)(2,1)S(1)} %copy-done.2), kind=kOutput, calls=%fused_computation.3 | convolution fusion | flops 8623489024 | bytes 134250496 | tf_op jit(solution)/shard_map/dot_general | solution.py:12
  3466.9 177.8 %copy.13 = bf16[64,64,64,128]{2,1,0,3:T(8,128)(2,1)} copy(bf16[64,64,64,128]{3,2,1,0:T(8,128)(2,1)} %convolution_convert_fusion) | data formatting | bytes 134217728 | tf_op jit(solution)/shard_map/convert_element_type | solution.py:12
  3644.7 112.2 %reshape.8 = bf16[2,2,8388608]{2,1,0:T(2,128)(2,1)} reshape(bf16[128,64,64,64]{3,2,1,0:T(8,128)(2,1)} %bitcast.29) | data formatting | bytes 134217728
  3756.9 110.3 %all_to_all.56 = bf16[2,2,8388608]{2,1,0:T(2,128)(2,1)} all-to-all(bf16[2,2,8388608]{2,1,0:T(2,128)(2,1)} %reshape.8), channel_id=1, replica_groups=mesh['dp'=1,'m3'=2,'m2'=2,'m1'=2] {'m1'}, dimensions={0} | all-to-all | bytes 134217728 | tf_op jit(solution)/shard_map/all_to_all | solution.py:13
  3867.2 172.2 %reshape.9 = bf16[128,64,64,64]{3,2,1,0:T(8,128)(2,1)} reshape(bf16[2,2,8388608]{2,1,0:T(2,128)(2,1)} %all_to_all.56) | data formatting | bytes 134217728
  4039.4 311.9 %copy.14 = bf16[64,64,64,2,64]{1,3,4,2,0:T(2,128)(2,1)} copy(bf16[64,64,64,2,64]{2,1,0,4,3:T(8,128)(2,1)} %bitcast.8) | data formatting | bytes 134217728 | tf_op jit(solution)/shard_map/all_to_all | solution.py:13
  4351.4 0.0 copy-start.1
  4351.4 0.0 copy-start.3
  4351.4 205.7 %all_to_all.50 = bf16[64,128,64,64]{1,3,2,0:T(8,128)(2,1)} reshape(bf16[64,2,64,64,64]{2,1,4,3,0:T(2,128)(2,1)} %bitcast.9) | data formatting | bytes 134217728 | tf_op jit(solution)/shard_map/all_to_all | solution.py:13
  4557.1 0.0 copy-done.1
  4557.1 0.0 copy-done.3
  4557.1 47.2 %multiply_convert_fusion = bf16[64,64,64,128]{3,2,1,0:T(8,128)(2,1)} fusion(f32[64,64,128]{2,1,0:T(8,128)S(1)} %copy-done.1, bf16[64,128,64,64]{1,3,2,0:T(8,128)(2,1)} %all_to_all.50, bf16[128,128]{1,0:T(8,128)(2,1)S(1)} %copy-done.3), kind=kOutput, calls=%fused_computation.2 | convolution fusion | flops 8724152320 | bytes 136347648 | tf_op jit(solution)/shard_map/dot_general | solution.py:14
Async XLA Ops:
  0.0 1687.3 %copy-start = (bf16[128,128]{1,0:T(8,128)(2,1)S(1)}, bf16[128,128]{1,0:T(8,128)(2,1)}, u32[]{:S(2)}) copy-start(bf16[128,128]{1,0:T(8,128)(2,1)} %param.8) | copy-start | bytes 98308
  3214.2 205.5 %copy-start.2 = (bf16[128,128]{1,0:T(8,128)(2,1)S(1)}, bf16[128,128]{1,0:T(8,128)(2,1)}, u32[]{:S(2)}) copy-start(bf16[128,128]{1,0:T(8,128)(2,1)} %param.7) | copy-start | bytes 98308
  4351.4 205.7 %copy-start.1 = (f32[64,64,128]{2,1,0:T(8,128)S(1)}, f32[64,64,128]{2,1,0:T(8,128)}, u32[]{:S(2)}) copy-start(f32[64,64,128]{2,1,0:T(8,128)} %param.9) | copy-start | bytes 6291460
  4351.4 205.7 %copy-start.3 = (bf16[128,128]{1,0:T(8,128)(2,1)S(1)}, bf16[128,128]{1,0:T(8,128)(2,1)}, u32[]{:S(2)}) copy-start(bf16[128,128]{1,0:T(8,128)(2,1)} %param.6) | copy-start | bytes 98308
where the time goes:
time: 4660 us; the launch traced here: 4600 us
  local copies, waits for them, and re-layouts  2790 us (60%)
  blocking collectives  1680 us (36%)
  matrix products  141 us (3%)
    unnamed x15, local copies, waits for them, and re-layouts  1030 us
    all_to_all x1, blocking collectives, local_step(): full_three = lax.all_to_all(vol_blk, 'm3', 0, 3, tiled=True)  784 us
    all_to_all x1, blocking collectives, local_step(): full_two = lax.all_to_all(prod_three, 'm2', 3, 2, tiled=True)  782 us
    all_to_all x2, local copies, waits for them, and re-layouts, local_step(): full_one = lax.all_to_all(prod_two, 'm1', 3, 1, tiled=True)  518 us
    all_to_all x2, local copies, waits for them, and re-layouts, local_step(): full_two = lax.all_to_all(prod_three, 'm2', 3, 2, tiled=True)  441 us
    all_to_all x2, local copies, waits for them, and re-layouts, local_step(): full_three = lax.all_to_all(vol_blk, 'm3', 0, 3, tiled=True)  441 us
    convert_element_type x1, local copies, waits for them, and re-layouts, local_step(): lax.dot_general(full_three, fac_three, (((3,), (1,)), ((), ())), preferre...  178 us
    convert_element_type x1, local copies, waits for them, and re-layouts, local_step(): lax.dot_general(full_two, fac_two, (((2,), (1,)), ((), ())), preferred_el...  178 us

commit v1 on v0

v1 whole, which is shorter than its diff:
```python
import functools

import jax
import jax.numpy as jnp
from jax import lax
from jax.experimental import pallas as pl
from jax.experimental.pallas import tpu as pltpu
from jax.sharding import PartitionSpec as P

MESH = pl.DeviceIdType.MESH
BF16, F32 = jnp.bfloat16, jnp.float32
UNITS = 128
AHEAD = 4
LAG = 6
PITCH = 24


def exchange_kernel(x_hbm, a3_ref, a2_ref, z_hbm, xbuf, pk, yr, xs, vo, vr, t3, t2, zo, zs,
                    x_sem, ys_sem, yr_sem, xs_sem, xr_sem, zl_sem, zs_sem, zr_sem, y_free, x_free, z_free):
    y, x, c = lax.axis_index("m3"), lax.axis_index("m2"), lax.axis_index("m1")

    barrier = pltpu.get_barrier_semaphore()
    for peer in ({"m3": 1 - y}, {"m2": 1 - x}, {"m1": 1 - c}):
        pl.semaphore_signal(barrier, inc=1, device_id=peer, device_id_type=MESH)
    pl.semaphore_wait(barrier, 3)

    def load(r):
        return pltpu.make_async_copy(
            x_hbm.at[pl.ds((r // 16) * 8, 8), pl.ds((r % 16) * 4, 4)], xbuf.at[r % 4], x_sem.at[r % 4])

    def pack(r):
        slot, part, quarter, pair = r % 4, (r // 16) % 2, (r // 4) % 4, (r % 4) * 2
        for a in range(8):
            for j in range(2):
                tile = xbuf[slot, a, 2 * j:2 * j + 2].reshape(128, 128).T
                for block in range(8):
                    pk[part, block // 4, block % 4, quarter, pair + j, a * 16:(a + 1) * 16, :] = (
                        tile[block * 16:(block + 1) * 16, :])

    def send_y(u):
        return pltpu.make_async_remote_copy(
            src_ref=pk.at[(u // 16) % 2, 1 - y, (u // 4) % 4, u % 4], dst_ref=yr.at[u % 8],
            send_sem=ys_sem.at[u % 8], recv_sem=yr_sem.at[u % 8], device_id={"m3": 1 - y}, device_id_type=MESH)

    def send_x(u):
        return pltpu.make_async_remote_copy(
            src_ref=xs.at[u % 4], dst_ref=vr.at[(u // 4) % 4, u % 4],
            send_sem=xs_sem.at[u % 4], recv_sem=xr_sem.at[(u // 4) % 4, u % 4],
            device_id={"m2": 1 - x}, device_id_type=MESH)

    def z_place(v):
        return z_hbm.at[pl.ds(((v // 4) % 4) * 16, 16), pl.ds((v % 4) * 8, 8), pl.ds(c * 64 + (v // 16) * 8, 8)]

    def keep_z(v):
        return pltpu.make_async_copy(zo.at[v % 4], z_place(v), zl_sem.at[v % 4])

    def send_z(v):
        return pltpu.make_async_remote_copy(
            src_ref=zs.at[v % 4], dst_ref=z_place(v), send_sem=zs_sem.at[v % 4], recv_sem=zr_sem.at[v % 4],
            device_id={"m1": 1 - c}, device_id_type=MESH)

    def product_three(u):
        part, group, quarter, slot = (u // 16) % 2, (u // 4) % 4, u % 4, u % 8
        chunk = (u // 4) % 4
        for pair in range(4):
            rows = []
            for j in range(2):
                own = pk[part, y, group, quarter, 2 * pair + j]
                other = yr[slot, 2 * pair + j]
                rows.append(jnp.concatenate([own, other], axis=1))
            prod = lax.dot_general(a3_ref[...], jnp.concatenate(rows, axis=0), (((1,), (1,)), ((), ())),
                                   preferred_element_type=F32)
            for j in range(2):
                for b in range(2):
                    t3[pl.ds((2 * pair + j) * 2 + b, 128, stride=PITCH), :] = (
                        prod[b * 128:(b + 1) * 128, j * 128:(j + 1) * 128])
        for k in range(64):
            vo[chunk, quarter, k] = t3[k * PITCH:k * PITCH + 16, :].astype(BF16)
        for k in range(64):
            xs[u % 4, k] = t3[(64 + k) * PITCH:(64 + k) * PITCH + 16, :].astype(BF16)

    def product_two(v):
        chunk, quarter, slot = (v // 4) % 4, v % 4, v % 4

        def pair(kk, carry):
            cols = []
            for j in range(2):
                k = (quarter * 8 + kk) * 2 + j
                cols.append(jnp.concatenate([vo[chunk, q, k] for q in range(4)] + [vr[chunk, q, k] for q in range(4)],
                                            axis=0))
            prod = jnp.dot(a2_ref[...], jnp.concatenate(cols, axis=1), preferred_element_type=F32)
            for h, out in enumerate((zo, zs)):
                turned = jnp.concatenate(
                    [prod[h * 64:(h + 1) * 64, :128], prod[h * 64:(h + 1) * 64, 128:]], axis=0).T
                for t in range(16):
                    t2[h, pl.ds((t % 2) * 64 + t // 2, 8, stride=8), :] = turned[t * 8:(t + 1) * 8, :]
                for s in range(16):
                    out[slot, s, kk] = t2[h, s * 8:(s + 1) * 8, :].astype(BF16)
            return carry

        lax.fori_loop(0, 8, pair, 0)

    for r in range(3):
        load(r).start()

    def prologue(r, carry):
        load(r).wait()
        load(r + 3).start()
        pack(r)

        @pl.when(r % 4 == 3)
        def _():
            send_y(r // 4).start()

        return carry

    lax.fori_loop(0, 16, prologue, 0)

    def step(m, carry):
        @pl.when(m < UNITS)
        def _():
            send_y(m).wait_recv()

            @pl.when(m >= 4)
            def _():
                send_x(m - 4).wait_send()

            product_three(m)
            send_y(m).wait_send()

            @pl.when(m < UNITS - 8)
            def _():
                pl.semaphore_signal(y_free, inc=1, device_id={"m3": 1 - y}, device_id_type=MESH)

        @pl.when(m < UNITS - 16)
        def _():
            r = m + 16
            load(r).wait()

            @pl.when(r < UNITS - 3)
            def _():
                load(r + 3).start()

            pack(r)

        @pl.when(m < UNITS - AHEAD)
        def _():
            @pl.when(m >= 4)
            def _():
                pl.semaphore_wait(y_free, 1)

            send_y(m + AHEAD).start()

        @pl.when(m < UNITS)
        def _():
            @pl.when((m % 4 == 0) & (m >= 16))
            def _():
                pl.semaphore_wait(x_free, 1)

            send_x(m).start()

        @pl.when(m >= LAG)
        def _():
            v = m - LAG

            @pl.when(v % 4 == 0)
            def _():
                for q in range(4):
                    send_x(v + q).wait_recv()

            @pl.when(v >= 4)
            def _():
                keep_z(v - 4).wait()
                send_z(v - 4).wait_send()
                pl.semaphore_wait(z_free, 1)

            product_two(v)

            @pl.when((v % 4 == 3) & (v < UNITS - 16))
            def _():
                pl.semaphore_signal(x_free, inc=1, device_id={"m2": 1 - x}, device_id_type=MESH)

            keep_z(v).start()
            send_z(v).start()

            @pl.when(v >= 2)
            def _():
                send_z(v - 2).wait_recv()

                @pl.when(v < UNITS - 2)
                def _():
                    pl.semaphore_signal(z_free, inc=1, device_id={"m1": 1 - c}, device_id_type=MESH)

        return carry

    lax.fori_loop(0, UNITS + LAG, step, 0)

    for u in range(UNITS - 4, UNITS):
        send_x(u).wait_send()
        keep_z(u).wait()
        send_z(u).wait_send()
    for u in range(UNITS - 2, UNITS):
        send_z(u).wait_recv()


def exchange(xt, a3, a2):
    flops = 2 * (512 * 256 * 256 * 256 + 32 * 64 * 128 * 128 * 128)
    return pl.pallas_call(
        exchange_kernel,
        name="exchange",
        out_shape=jax.ShapeDtypeStruct((64, 32, 128, 128), BF16),
        in_specs=[pl.BlockSpec(memory_space=pl.ANY), pl.BlockSpec(memory_space=pltpu.VMEM),
                  pl.BlockSpec(memory_space=pltpu.VMEM)],
        out_specs=pl.BlockSpec(memory_space=pl.ANY),
        scratch_shapes=[
            pltpu.VMEM((4, 8, 4, 64, 128), BF16),
            pltpu.VMEM((2, 2, 4, 4, 8, 128, 128), BF16),
            pltpu.VMEM((8, 8, 128, 128), BF16),
            pltpu.VMEM((4, 64, 16, 128), BF16),
            pltpu.VMEM((4, 4, 64, 16, 128), BF16),
            pltpu.VMEM((4, 4, 64, 16, 128), BF16),
            pltpu.VMEM((128 * PITCH, 128), F32),
            pltpu.VMEM((2, 128, 128), F32),
            pltpu.VMEM((4, 16, 8, 8, 128), BF16),
            pltpu.VMEM((4, 16, 8, 8, 128), BF16),
            pltpu.SemaphoreType.DMA((4,)),
            pltpu.SemaphoreType.DMA((8,)),
            pltpu.SemaphoreType.DMA((8,)),
            pltpu.SemaphoreType.DMA((4,)),
            pltpu.SemaphoreType.DMA((4, 4)),
            pltpu.SemaphoreType.DMA((4,)),
            pltpu.SemaphoreType.DMA((4,)),
            pltpu.SemaphoreType.DMA((4,)),
            pltpu.SemaphoreType.REGULAR,
            pltpu.SemaphoreType.REGULAR,
            pltpu.SemaphoreType.REGULAR,
        ],
        cost_estimate=pl.CostEstimate(flops=flops, bytes_accessed=2 * 64 * 2**20, transcendentals=0),
        compiler_params=pltpu.CompilerParams(collective_id=0, has_side_effects=True, vmem_limit_bytes=62 * 2**20),
    )(xt, a3, a2)


def last_kernel(z_ref, a1_ref, d_ref, w_ref):
    for kk in range(32):
        prod = lax.dot_general(z_ref[0, kk], a1_ref[...], (((0,), (1,)), ((), ())), preferred_element_type=F32)
        scale = d_ref[2 * kk:2 * kk + 2].reshape(128, 128)
        w_ref[0, 2 * kk:2 * kk + 2] = (scale * prod.astype(BF16).astype(F32)).astype(BF16).reshape(2, 64, 128)


def last_product(z, a1, d):
    return pl.pallas_call(
        last_kernel,
        name="last_product",
        grid=(64,),
        out_shape=jax.ShapeDtypeStruct((64, 64, 64, 128), BF16),
        in_specs=[pl.BlockSpec((1, 32, 128, 128), lambda s: (s, 0, 0, 0)), pl.BlockSpec((128, 128), lambda s: (0, 0)),
                  pl.BlockSpec((64, 64, 128), lambda s: (0, 0, 0))],
        out_specs=pl.BlockSpec((1, 64, 64, 128), lambda s: (s, 0, 0, 0)),
        cost_estimate=pl.CostEstimate(flops=2 * 64 * 4096 * 128 * 128, bytes_accessed=2 * 64 * 2**20, transcendentals=0),
        compiler_params=pltpu.CompilerParams(vmem_limit_bytes=32 * 2**20),
    )(z, a1, d)


def solution(mesh):
    def local_step(vol_blk, fac_one, fac_two, fac_three, diag_blk):
        y, x, c = lax.axis_index("m3"), lax.axis_index("m2"), lax.axis_index("m1")

        def own_first(mat, index, axis):
            return jnp.where(index == 0, mat, jnp.roll(mat, 64, axis))

        three = own_first(own_first(fac_three, x, 0), y, 1)
        three = jnp.einsum("bc,ksl->bkscl", jnp.eye(2, dtype=BF16), three.reshape(128, 2, 64)).reshape(256, 256)
        two = own_first(own_first(fac_two, c, 0), x, 1)
        z = exchange(jnp.transpose(vol_blk, (1, 2, 3, 0)), three, two)
        return last_product(z, fac_one, diag_blk)

    return jax.shard_map(local_step, mesh=mesh, in_specs=(P("dp", "m1", "m2", "m3"), P(), P(), P(), P("m2", "m1", None)),
                         out_specs=P(("dp", "m3"), "m2", "m1", None), check_vma=False)
```

time: 4660 us -> 837 us (0.18); the launches traced: 4600 us -> 834 us
  local copies, waits for them, and re-layouts: 2790 us -> 4.12 us
  blocking collectives: 1680 us -> 0 us
  Pallas kernels: 0 us -> 828 us
  matrix products: 141 us -> 0 us
    all_to_all x3 -> x0, blocking collectives: 1680 us -> none  [the longest x1 784 us: local_step(): full_three = lax.all_to_all(vol_blk, 'm3', 0, 3, tiled=True)]
    all_to_all x6 -> x0, local copies, waits for them, and re-layouts: 1400 us -> none  [the longest x2 518 us: local_step(): full_one = lax.all_to_all(prod_two, 'm1', 3, 1, tiled=True)]
    unnamed x15 -> x5, local copies, waits for them, and re-layouts: 1030 us -> 1.61 us
    pallas_call x0 -> x2, Pallas kernels: none -> 828 us  [the longest x1 744 us: exchange(): pl.pallas_call(exchange_kernel, name='exchange', out_shape=jax.ShapeDtype...]
    convert_element_type x2 -> x0, local copies, waits for them, and re-layouts: 356 us -> none  [the longest x1 178 us: local_step(): lax.dot_general(full_three, fac_three, (((3,), (1,)), ((), ())), preferre...]
    dot_general x3 -> x0, matrix products: 141 us -> none  [the longest x1 47.2 us: local_step(): lax.dot_general(full_one, fac_one, (((1,), (1,)), ((), ())), preferred_el...]
where the time goes in v1:
time: 837 us; the launch traced here: 834 us
  Pallas kernels  828 us (99%)
    pallas_call x1, Pallas kernels, exchange(): pl.pallas_call(exchange_kernel, name='exchange', out_shape=jax.ShapeDtype...  744 us
    pallas_call x1, Pallas kernels, last_product(): pl.pallas_call(last_kernel, name='last_product', grid=(64,), out_shape=ja...  83.3 us

profile of v1, /device:TPU:0, one launch (start us, length us, event | category | flops | bytes accessed | tf_op | source)
XLA Modules:
  0.0 834.3 jit_solution(16028569777357555258)
XLA Ops:
  0.0 0.7 fusion.1
  0.7 0.8 maximum_select_fusion.2
  1.5 0.7 fusion.3
  2.3 0.1 fusion
  2.3 1.5 maximum_select_fusion
  3.8 0.1 fusion.2
  3.9 0.1 maximum_select_fusion.1
  4.0 0.1 copy.6
  4.1 0.2 broadcast_multiply_fusion
  4.3 0.8 copy.7.a3_ref
  5.0 0.0 copy-start.1
  5.1 744.4 %exchange.1.z_ref = bf16[64,32,128,128]{3,2,1,0:T(8,128)(2,1)} custom-call(bf16[64,64,64,128]{3,2,1,0:T(8,128)(2,1)} %bitcast.x_hbm, bf16[256,256]{1,0:T(8,128)(2,1)} %copy.7.a3_ref, bf16[128,128]{1,0:T(8,128)(2,1)} %get-tuple-element.14.a2_ref), custom_call_target="tpu_custom_call" | custom-call | flops 25769803776 | bytes 134217728 | tf_op jit(solution)/shard_map/exchange/pallas_call | solution.py:208
  749.5 0.0 copy-done.1
  749.5 0.0 copy-start
  749.5 1.6 copy-done
  751.1 83.3 %last_product.1 = bf16[64,64,64,128]{3,2,1,0:T(8,128)(2,1)} custom-call(bf16[64,32,128,128]{3,2,1,0:T(8,128)(2,1)} %exchange.1.z_ref, bf16[128,128]{1,0:T(8,128)(2,1)S(1)} %copy-done.1, f32[64,64,128]{2,1,0:T(8,128)S(1)} %copy-done), custom_call_target="tpu_custom_call" | custom-call | flops 8589934592 | bytes 134217728 | tf_op jit(solution)/shard_map/last_product/pallas_call | solution.py:251
  (2 shorter events, 0.0 us)
Async XLA Ops:
  5.0 744.4 %copy-start.1 = (bf16[128,128]{1,0:T(8,128)(2,1)S(1)}, bf16[128,128]{1,0:T(8,128)(2,1)}, u32[]{:S(2)}) copy-start(bf16[128,128]{1,0:T(8,128)(2,1)} %a1_ref.1) | copy-start | bytes 98308
  749.5 1.6 copy-start
